TPU v7x, 32 devices: a whole 2x2x4 slice. The times are simulated.
32 devices in a mesh: seq: 4 (over x, core), fsdp: 8 (over z, y).
Axes of the slice: x: 2, y: 2, z: 4, core: 2. Of those that a mesh axis runs over, the one named last changes fastest.
Arguments:
- bytes_in: bfloat16 [4, 2048, 1280], P('seq', 'fsdp'), may hold values from -12 to 12, as said below
- doc_lengths: int32 [8], replicated, may hold values from 1 to 2048, 8192 in all
- patch_offsets: int32 [4, 512], P('seq', 'fsdp'), may hold values from 0 to 256, as said below
- patch_counts: int32 [4, 8], P('seq', 'fsdp'), may hold values from 32 to 64, as said below
- w_query: bfloat16 [1280, 1280], replicated, may hold values from -0.15625 to 0.15625
- w_key: bfloat16 [1280, 1280], replicated, may hold values from -0.15625 to 0.15625
- w_value: bfloat16 [1280, 1280], replicated, may hold values from -0.15625 to 0.15625
- w_proj: bfloat16 [1280, 4096], replicated, may hold values from -0.15625 to 0.15625
- norm_gain: float32 [4096], replicated, may hold values from 0.1 to 1.9
- gate_w: bfloat16 [4096, 7168], P('fsdp', 'seq'), may hold values from -0.09375 to 0.09375
- up_w: bfloat16 [4096, 7168], P('fsdp', 'seq'), may hold values from -0.09375 to 0.09375
- d_hidden: bfloat16 [4, 512, 7168], P(None, 'fsdp', 'seq'), may hold values from -6 to 6
Outputs:
- hidden: bfloat16 [4, 512, 7168], P(None, 'fsdp', 'seq')
- grad_gate: float32 [4096, 7168], P('fsdp', 'seq')
- grad_up: float32 [4096, 7168], P('fsdp', 'seq')
- d_patches: float32 [4, 512, 4096], P('seq', 'fsdp')
Inputs may be any that keep to these rules, and one draw needn't show every extreme that they name: `bytes_in`: byte states of order one. `patch_offsets`: in each device block of 64 slots, slot 0 holds 0, the first c slots hold strictly rising offsets, c being the block's entry of patch_counts, and the other slots hold 256. `patch_counts`: patches of one device block; 64 is reached by some block in every draw.
All inputs are finite; a program needn't handle non-finite values.
Results may differ from a plain program's by a relative error of at most 0.022.
Values may be sent and summed in bfloat16 or wider, within the bound.
No kernel may reach another device: no remote copies, remote signals or barrier semaphores. Data moves between devices by JAX's collectives and lax.ppermute only.
A program may use at most 192 MiB of HBM per device.

v0:
```python
import math

import jax
import jax.numpy as jnp
from jax import lax
from jax.sharding import PartitionSpec as P

HEAD = 128
WINDOW = 512


epsilon = 1e-05
masked_score = -1e30


def shifted(shard, axis, by):
    devices = lax.axis_size(axis)
    pairs = [(i, i + by) for i in range(devices) if 0 <= i + by < devices]
    return lax.ppermute(shard, axis, pairs)


def doc_index(doc_lengths, positions):
    starts = jnp.cumsum(doc_lengths) - doc_lengths
    inside = (starts[None, :] <= positions[:, None]).astype(jnp.int32)
    return jnp.sum(inside, axis=1) - 1


def window_attention(queries, key_rows, values, query_pos, key_pos, query_doc, key_doc):
    row_count = queries.shape[0]
    head_count = queries.shape[1] // HEAD
    query_heads = queries.reshape(row_count, head_count, HEAD)
    key_heads = key_rows.reshape(-1, head_count, HEAD)
    value_heads = values.reshape(-1, head_count, HEAD)
    scores = jnp.einsum(
        "qhd,khd->hqk", query_heads, key_heads, preferred_element_type=jnp.float32
    ) / math.sqrt(HEAD)
    allowed = (key_pos[None, :] <= query_pos[:, None]) & (
        query_pos[:, None] - key_pos[None, :] < WINDOW
    )
    allowed = allowed & (key_pos[None, :] >= 0) & (key_doc[None, :] == query_doc[:, None])
    scores = jnp.where(allowed[None], scores, masked_score)
    row_max = jnp.max(scores, axis=-1, keepdims=True)
    weights = jnp.exp(scores - row_max)
    weights = (weights / jnp.sum(weights, axis=-1, keepdims=True)).astype(jnp.bfloat16)
    mixed = jnp.einsum("hqk,khd->qhd", weights, value_heads, preferred_element_type=jnp.float32)
    return mixed.reshape(row_count, head_count * HEAD)


def pool_patches(states, offsets, count):
    length = states.shape[0]
    slot_count = offsets.shape[0]
    head_count = states.shape[1] // HEAD
    slot_ids = jnp.arange(slot_count, dtype=jnp.int32)
    present = slot_ids < count
    following = jnp.concatenate([offsets[1:], jnp.full((1,), length, jnp.int32)])
    patch_ends = jnp.where(slot_ids == count - 1, length, following)
    byte_ids = jnp.arange(length, dtype=jnp.int32)
    member = (
        present[:, None]
        & (offsets[:, None] <= byte_ids[None, :])
        & (byte_ids[None, :] < patch_ends[:, None])
    )
    patch_sizes = jnp.sum(member.astype(jnp.float32), axis=1, keepdims=True)
    summed = jnp.dot(member.astype(jnp.bfloat16), states, preferred_element_type=jnp.float32)
    pooled = (summed / jnp.maximum(patch_sizes, 1.0)).astype(jnp.bfloat16)
    pooled_heads = pooled.reshape(slot_count, head_count, HEAD)
    state_heads = states.reshape(length, head_count, HEAD)
    scores = jnp.einsum(
        "jhd,bhd->hjb", pooled_heads, state_heads, preferred_element_type=jnp.float32
    ) / math.sqrt(HEAD)
    scores = jnp.where(member[None], scores, masked_score)
    row_max = jnp.max(scores, axis=-1, keepdims=True)
    weights = jnp.exp(scores - row_max)
    weights = (weights / jnp.sum(weights, axis=-1, keepdims=True)).astype(jnp.bfloat16)
    context = jnp.einsum("hjb,bhd->jhd", weights, state_heads, preferred_element_type=jnp.float32)
    context = context.reshape(slot_count, head_count * HEAD)
    return jnp.where(present[:, None], context, 0.0).astype(jnp.bfloat16)


def shards(
    bytes_in,
    doc_lengths,
    patch_offsets,
    patch_counts,
    w_query,
    w_key,
    w_value,
    w_proj,
    norm_gain,
    gate_w,
    up_w,
    d_hidden,
):
    states = bytes_in[0]
    length = states.shape[0]
    hop_count = (WINDOW - 2 + length) // length
    first_pos = lax.axis_index(("seq", "fsdp")) * length
    queries = jnp.dot(states, w_query, preferred_element_type=jnp.float32).astype(jnp.bfloat16)
    key_rows = jnp.dot(states, w_key, preferred_element_type=jnp.float32).astype(jnp.bfloat16)
    values = jnp.dot(states, w_value, preferred_element_type=jnp.float32).astype(jnp.bfloat16)
    key_parts = [key_rows]
    value_parts = [values]
    for distance in range(1, hop_count + 1):
        earlier_keys, earlier_values = shifted((key_rows, values), ("seq", "fsdp"), distance)
        key_parts.insert(0, earlier_keys)
        value_parts.insert(0, earlier_values)
    key_all = jnp.concatenate(key_parts, axis=0)
    value_all = jnp.concatenate(value_parts, axis=0)
    query_pos = first_pos + jnp.arange(length, dtype=jnp.int32)
    key_pos = first_pos - hop_count * length + jnp.arange((hop_count + 1) * length, dtype=jnp.int32)
    key_doc = doc_index(doc_lengths, key_pos)
    query_doc = key_doc[hop_count * length :]
    mixed = window_attention(queries, key_all, value_all, query_pos, key_pos, query_doc, key_doc)
    hidden_bytes = (states.astype(jnp.float32) + mixed).astype(jnp.bfloat16)
    context = pool_patches(hidden_bytes, patch_offsets[0], patch_counts[0, 0])
    seq_index = lax.axis_index("seq")
    shard_part = lax.all_gather(context[None], "seq", axis=0, tiled=True)
    flat_part = shard_part.reshape(-1, shard_part.shape[-1])
    result = jnp.dot(flat_part, w_proj, preferred_element_type=jnp.float32).astype(jnp.bfloat16)
    features = result.reshape(shard_part.shape[0], shard_part.shape[1], -1)
    seq_count, slot_count, model_width = features.shape
    patch_float = features.reshape(seq_count * slot_count, model_width).astype(jnp.float32)
    inverse = lax.rsqrt(jnp.mean(patch_float * patch_float, axis=1, keepdims=True) + epsilon)
    normed = (patch_float * inverse * norm_gain).astype(jnp.bfloat16)
    gate_full, up_full = (
        lax.all_gather(gate_w, "fsdp", axis=0, tiled=True),
        lax.all_gather(up_w, "fsdp", axis=0, tiled=True),
    )
    gate_pre = jnp.dot(normed, gate_full, preferred_element_type=jnp.float32)
    up_pre = jnp.dot(normed, up_full, preferred_element_type=jnp.float32)
    sigmoid_gate = jax.nn.sigmoid(gate_pre)
    hidden = (gate_pre * sigmoid_gate * up_pre).astype(jnp.bfloat16)
    units = gate_w.shape[1]
    cotangent = d_hidden.reshape(seq_count * slot_count, units).astype(jnp.float32)
    gate_grad = (
        cotangent * up_pre * sigmoid_gate * (1.0 + gate_pre * (1.0 - sigmoid_gate))
    ).astype(jnp.bfloat16)
    up_grad = (cotangent * gate_pre * sigmoid_gate).astype(jnp.bfloat16)
    both_grads = jnp.concatenate([gate_grad, up_grad], axis=1)
    weight_partial = lax.dot_general(
        normed, both_grads, (((0,), (0,)), ((), ())), preferred_element_type=jnp.float32
    )
    reduced = lax.psum_scatter(
        weight_partial.astype(jnp.bfloat16), "fsdp", scatter_dimension=0, tiled=True
    ).astype(jnp.float32)
    grad_gate = reduced[:, :units]
    grad_up = reduced[:, units:]
    input_partial = lax.dot_general(
        gate_grad, gate_full, (((1,), (1,)), ((), ())), preferred_element_type=jnp.float32
    )
    input_partial = input_partial + lax.dot_general(
        up_grad, up_full, (((1,), (1,)), ((), ())), preferred_element_type=jnp.float32
    )
    normed_grad = lax.psum_scatter(
        input_partial.reshape(seq_count, slot_count, model_width).astype(jnp.bfloat16),
        "seq",
        scatter_dimension=0,
        tiled=True,
    ).astype(jnp.float32)[0]
    own_float = lax.dynamic_index_in_dim(
        patch_float.reshape(seq_count, slot_count, model_width), seq_index, 0, keepdims=False
    )
    own_inverse = lax.dynamic_index_in_dim(
        inverse.reshape(seq_count, slot_count, 1), seq_index, 0, keepdims=False
    )
    scaled = norm_gain * normed_grad
    patch_grad = own_inverse * scaled - own_float * (
        own_inverse * own_inverse * own_inverse
    ) * jnp.mean(scaled * own_float, axis=1, keepdims=True)
    return (hidden.reshape(seq_count, slot_count, units), grad_gate, grad_up, patch_grad[None])


def solution(mesh):
    return jax.shard_map(
        shards,
        mesh=mesh,
        in_specs=(
            P("seq", "fsdp", None),
            P(),
            P("seq", "fsdp"),
            P("seq", "fsdp"),
            P(),
            P(),
            P(),
            P(),
            P(),
            P("fsdp", "seq"),
            P("fsdp", "seq"),
            P(None, "fsdp", "seq"),
        ),
        out_specs=(
            P(None, "fsdp", "seq"),
            P("fsdp", "seq"),
            P("fsdp", "seq"),
            P("seq", "fsdp", None),
        ),
        check_vma=False,
    )
```

profile of v0, /device:TPU:0, one launch (start us, length us, event | category | flops | bytes accessed | tf_op | source)
XLA Modules:
  0.0 1013.8 jit_solution(9072286040798609291)
XLA Ops:
  7.2 0.7 all-gather.3.cloned.1.call-update
  8.0 0.7 all-gather.5.cloned.1.call-update
  8.7 0.4 copy-done
  9.1 3.1 convolution_convert_fusion.2
  12.2 5.1 collective-permute-start.2
  17.3 4.3 collective-permute-start.3
  21.6 1.9 convolution_convert_fusion.4
  23.5 3.5 collective-permute-start
  26.9 4.3 collective-permute-start.1
  31.9 0.2 reduce-window.9
  32.3 0.2 convert_reduce_fusion
  32.7 3.0 convolution_convert_fusion.3
  35.7 1.3 copy.46
  37.0 0.2 copy.48
  37.2 0.3 fusion.30
  37.6 4.4 collective-permute-done.2
  42.0 0.8 copy-done.6
  42.9 6.6 collective-permute-done.3
  49.5 1.6 pad_maximum_fusion.1
  51.1 2.3 copy.49
  53.4 15.6 %collective-permute-done = bf16[256,1280]{1,0:T(8,128)(2,1)} collective-permute-done((bf16[256,1280]{1,0:T(8,128)(2,1)}, bf16[256,1280]{1,0:T(8,128)(2,1)}, u32[]{:S(2)}, u32[]{:S(2)}) %collective-permute-start) | collective-permute-done | bytes 655392 | tf_op jit(solution)/shard_map/ppermute | solution.py:19
  69.0 1.6 pad_maximum_fusion
  70.6 2.3 copy.47
  72.9 7.8 fusion.48
  80.7 6.2 fusion.19
  86.9 1.7 copy.52
  88.6 0.3 fusion.22
  88.9 0.2 fusion.21
  89.2 0.3 fusion.49
  89.4 1.2 convolution_bitcast_fusion
  90.6 0.1 copy.56
  91.0 69.2 %all_gather.9 = bf16[4,64,1280]{2,1,0:T(8,128)(2,1)S(1)} all-gather(bf16[1,64,1280]{2,1,0:T(8,128)(2,1)S(1)} %select_convert_fusion), channel_id=1, replica_groups=mesh['seq'=4,'fsdp'=8] {'seq'}, dimensions={0}, use_global_device_ids=true | all-gather | bytes 819200 | tf_op jit(solution)/shard_map/all_gather | solution.py:117
  160.2 5.8 multiply_reduce_fusion
  166.0 1.9 copy-done.2
  167.9 0.6 multiply_convert_fusion
  168.5 94.8 %all-gather.3.cloned.1.call-done = bf16[4096,1792]{1,0:T(8,128)(2,1)} async-done(((bf16[512,1792]{1,0:T(8,128)(2,1)}), bf16[4096,1792]{1,0:T(8,128)(2,1)}) %all-gather.3.cloned.1.call-update) | async-done | bytes 14680080 | tf_op jit(solution)/shard_map/all_gather | solution.py:126
  263.3 8.5 fusion.50
  271.8 193.6 %all-gather.5.cloned.1.call-done = bf16[4096,1792]{1,0:T(8,128)(2,1)} async-done(((bf16[512,1792]{1,0:T(8,128)(2,1)}), bf16[4096,1792]{1,0:T(8,128)(2,1)}) %all-gather.5.cloned.1.call-update) | async-done | bytes 14680080 | tf_op jit(solution)/shard_map/all_gather | solution.py:127
  465.4 11.3 %fusion.12 = (bf16[256,1792]{1,0:T(8,128)(2,1)S(1)}, bf16[256,1792]{1,0:T(8,128)(2,1)}, bf16[256,1792]{1,0:T(8,128)(2,1)}) fusion(f32[256,1792]{1,0:T(8,128)} %fusion.50, bf16[4,64,1792]{2,1,0:T(8,128)(2,1)} %param.23, bf16[256,4096]{1,0:T(8,128)(2,1)S(1)} %multiply_convert_fusion, bf16[4096,1792]{1,0:T(8,128)(2,1)} %all-gather.5.cloned.1.call-done), kind=kOutput, calls=%fused_computation.28 | convolution fusion | flops 3765895168 | bytes 22282240 | tf_op jit(solution)/shard_map/dot_general | solution.py:130
  476.7 16.0 %fusion.51 = f32[256,4096]{1,0:T(8,128)} fusion(bf16[256,1792]{1,0:T(8,128)(2,1)S(1)} %get-tuple-element.8, bf16[4096,1792]{1,0:T(8,128)(2,1)} %all-gather.3.cloned.1.call-done), kind=kOutput, calls=%fused_computation.93 | convolution fusion | flops 3758096384 | bytes 19791872 | tf_op jit(solution)/shard_map/dot_general | solution.py:148
  492.7 12.0 %fusion.3 = bf16[256,4096]{1,0:T(8,128)(2,1)} fusion(f32[256,4096]{1,0:T(8,128)} %fusion.51, bf16[256,1792]{1,0:T(8,128)(2,1)} %get-tuple-element.10, bf16[4096,1792]{1,0:T(8,128)(2,1)} %all-gather.5.cloned.1.call-done), kind=kOutput, calls=%fused_computation.8 | convolution fusion | flops 3760193536 | bytes 21889024 | tf_op jit(solution)/shard_map/dot_general | solution.py:151
  504.8 0.3 reduce-scatter.3.cloned.1.call-start
  505.0 13.8 %convolution_convert_fusion = bf16[4096,3584]{1,0:T(8,128)(2,1)} fusion(bf16[256,4096]{1,0:T(8,128)(2,1)S(1)} %multiply_convert_fusion, bf16[256,1792]{1,0:T(8,128)(2,1)} %get-tuple-element.10, bf16[256,1792]{1,0:T(8,128)(2,1)S(1)} %get-tuple-element.8), kind=kOutput, calls=%fused_computation.2 | convolution fusion | flops 7534542848 | bytes 33292288 | tf_op jit(solution)/shard_map/dot_general | solution.py:140
  519.0 15.3 %reduce-scatter.5.cloned.1.call-done = bf16[1,64,4096]{2,1,0:T(8,128)(2,1)} async-done(((bf16[4,64,4096]{2,1,0:T(8,128)(2,1)}), bf16[1,64,4096]{2,1,0:T(8,128)(2,1)}) %reduce-scatter.5.cloned.1.call-update) | async-done | bytes 524304 | tf_op jit(solution)/shard_map/reduce_scatter | solution.py:154
  534.3 1.6 fusion.27
  535.9 2.6 fusion.24
  538.5 462.9 %reduce-scatter.3.cloned.1.call-done = bf16[512,3584]{1,0:T(8,128)(2,1)} async-done(((bf16[4096,3584]{1,0:T(8,128)(2,1)}), bf16[512,3584]{1,0:T(8,128)(2,1)}) %reduce-scatter.3.cloned.1.call-update) | async-done | bytes 3670032 | tf_op jit(solution)/shard_map/reduce_scatter | solution.py:143
  1001.5 5.8 fusion.47
  (43 shorter events, 0.9 us)
Async XLA Ops:
  7.2 1.9 copy-start
  7.2 256.1 %all-gather.3.cloned.1.call-start = ((), (), s32[]{:S(2)}) async-start(), calls=%async_computation.2 | async-start | bytes 16515072 | tf_op jit(solution)/shard_map/all_gather | solution.py:126
  7.9 457.5 %all-gather.5.cloned.1.call-start = ((), (), s32[]{:S(2)}) async-start(), calls=%async_computation.3 | async-start | bytes 16515072 | tf_op jit(solution)/shard_map/all_gather | solution.py:127
  8.7 525.6 %reduce-scatter.5.cloned.1.call-start = ((), (), s32[]{:S(2)}) async-start(), calls=%async_computation.5 | async-start | bytes 2621440 | tf_op jit(solution)/shard_map/reduce_scatter | solution.py:154
  9.1 12.5 %copy-start.3 = (bf16[1,256,1280]{2,1,0:T(8,128)(2,1)S(1)}, bf16[1,256,1280]{2,1,0:T(8,128)(2,1)}, u32[]{:S(2)}) copy-start(bf16[1,256,1280]{2,1,0:T(8,128)(2,1)} %param.12) | copy-start | bytes 1966084
  9.1 12.5 %copy-start.9 = (bf16[1280,1280]{1,0:T(8,128)(2,1)S(1)}, bf16[1280,1280]{1,0:T(8,128)(2,1)}, u32[]{:S(2)}) copy-start(bf16[1280,1280]{1,0:T(8,128)(2,1)} %param.18) | copy-start | bytes 9830404
  12.2 19.7 %copy-start.10 = (s32[8]{0:T(128)S(1)}, s32[8]{0:T(128)}, u32[]{:S(2)}) copy-start(s32[8]{0:T(128)} %param.13) | copy-start | bytes 100
  12.2 19.9 %copy-start.8 = (s32[1,64]{1,0:T(1,128)S(1)}, s32[1,64]{1,0:T(1,128)}, u32[]{:S(2)}) copy-start(s32[1,64]{1,0:T(1,128)} %param.14) | copy-start | bytes 772
  12.2 20.4 %copy-start.4 = (bf16[1,256,1280]{2,1,0:T(8,128)(2,1)S(1)}, bf16[1,256,1280]{2,1,0:T(8,128)(2,1)}, u32[]{:S(2)}) copy-start(bf16[1,256,1280]{2,1,0:T(8,128)(2,1)} %param.12) | copy-start | bytes 1966084
  12.2 29.8 %collective-permute-start.2 = (bf16[256,1280]{1,0:T(8,128)(2,1)}, bf16[256,1280]{1,0:T(8,128)(2,1)S(1)}, u32[]{:S(2)}, u32[]{:S(2)}) collective-permute-start(bf16[256,1280]{1,0:T(8,128)(2,1)} %convolution_convert_fusion.2), channel_id=1, source_target_pairs={{0,2},{1,3},{2,4},{3,5},{4,6},{5,7},{6,8},{7,9},{8,10},{9,11},{10,... | collective-permute-start | bytes 1966088 | tf_op jit(solution)/shard_map/ppermute | solution.py:19
  17.3 32.2 %collective-permute-start.3 = (bf16[256,1280]{1,0:T(8,128)(2,1)}, bf16[256,1280]{1,0:T(8,128)(2,1)}, u32[]{:S(2)}, u32[]{:S(2)}) collective-permute-start(bf16[256,1280]{1,0:T(8,128)(2,1)} %convolution_convert_fusion.2), channel_id=1, source_target_pairs={{0,1},{1,2},{2,3},{3,4},{4,5},{5,6},{6,7},{7,8},{8,9},{9,10},{10,1... | collective-permute-start | bytes 1966088 | tf_op jit(solution)/shard_map/ppermute | solution.py:19
  23.5 45.5 %collective-permute-start = (bf16[256,1280]{1,0:T(8,128)(2,1)}, bf16[256,1280]{1,0:T(8,128)(2,1)}, u32[]{:S(2)}, u32[]{:S(2)}) collective-permute-start(bf16[256,1280]{1,0:T(8,128)(2,1)} %convolution_convert_fusion.4), channel_id=1, source_target_pairs={{0,2},{1,3},{2,4},{3,5},{4,6},{5,7},{6,8},{7,9},{8,10},{9,11},{10,... | collective-permute-start | bytes 1966088 | tf_op jit(solution)/shard_map/ppermute | solution.py:19
  26.9 42.0 %collective-permute-start.1 = (bf16[256,1280]{1,0:T(8,128)(2,1)}, bf16[256,1280]{1,0:T(8,128)(2,1)}, u32[]{:S(2)}, u32[]{:S(2)}) collective-permute-start(bf16[256,1280]{1,0:T(8,128)(2,1)} %convolution_convert_fusion.4), channel_id=1, source_target_pairs={{0,1},{1,2},{2,3},{3,4},{4,5},{5,6},{6,7},{7,8},{8,9},{9,10},{10,1... | collective-permute-start | bytes 1966088 | tf_op jit(solution)/shard_map/ppermute | solution.py:19
  42.0 0.8 copy-start.6
  72.9 7.8 copy-start.5
  160.2 7.7 copy-start.7
  166.0 1.9 copy-start.2
  504.8 496.7 %reduce-scatter.3.cloned.1.call-start = ((), (), s32[]{:S(2)}) async-start(), calls=%async_computation.4 | async-start | bytes 33030144 | tf_op jit(solution)/shard_map/reduce_scatter | solution.py:143
  1001.5 5.8 copy-start.1
Sparse Core Ops, SparseCore 0:
  10.2 253.0 all-gather.2
  265.5 199.8 all-gather.4
  504.9 29.3 reduce-scatter.4
  538.0 463.4 reduce-scatter.2
where the time goes:
time: 1010 us
  waiting for transfers between devices  795 us (79%)
  matrix products  91 us (9%)
  blocking collectives  69.2 us (7%)
  starting transfers between devices  17.5 us (2%)
  local copies, waits for them, and re-layouts  17.2 us (2%)
  between operations  14.6 us (1%)
    reduce_scatter x1, waiting for transfers between devices, shards(): lax.psum_scatter(weight_partial.astype(jnp.bfloat16), 'fsdp', scatter_dim...  463 us
    all_gather x1, waiting for transfers between devices, shards(): lax.all_gather(up_w, 'fsdp', axis=0, tiled=True)  194 us
    all_gather x1, waiting for transfers between devices, shards(): lax.all_gather(gate_w, 'fsdp', axis=0, tiled=True)  94.8 us
    all_gather x1, blocking collectives, shards(): shard_part = lax.all_gather(context[None], 'seq', axis=0, tiled=True)  69.2 us
    ppermute x4, waiting for transfers between devices, shifted(): return lax.ppermute(shard, axis, pairs)  26.7 us
  transfers between devices with their start and end apart: 8, of which 7 were waited for; matrix products, arithmetic and copies ran while one was open for 7% of the time, Pallas kernels for 0%

commit v1 on v0

v1 whole, which is shorter than its diff:
```python
import math

import jax
import jax.numpy as jnp
from jax import lax
from jax.experimental import pallas as pl
from jax.experimental.pallas import tpu as pltpu
from jax.sharding import Mesh
from jax.sharding import PartitionSpec as P


HEAD = 128
WINDOW = 512


epsilon = 1e-05
masked_score = -1e30


ROW_AXES = ("x", "core")
COL_AXES = ("a", "c", "b")
ALL_AXES = ROW_AXES + COL_AXES
CHUNK = 256


def shifted(shard, axis, by):
    devices = lax.axis_size(axis)
    pairs = [(i, i + by) for i in range(devices) if 0 <= i + by < devices]
    return lax.ppermute(shard, axis, pairs)


def turned(shard, axis, by):
    devices = lax.axis_size(axis)
    if by % devices == 0:
        return shard
    return lax.ppermute(shard, axis, [(i, (i + by) % devices) for i in range(devices)])


def chosen(blocks, index):
    result = blocks[0]
    for k in range(1, len(blocks)):
        result = jnp.where(index == k, blocks[k], result)
    return result


def split(array, count, dim):
    return jnp.split(array, count, axis=dim) if count > 1 else [array]


def after(value, *others):
    return lax.optimization_barrier((value, *others))[0]


def own_sum(partial, axis, dim, order=None):
    devices = lax.axis_size(axis)
    blocks = split(partial, devices, dim)
    total = blocks[0].astype(jnp.float32)
    for k in range(1, devices):
        sent = blocks[k].astype(jnp.bfloat16)
        if order is not None:
            sent = order(sent, k)
        total = total + turned(sent, axis, -k).astype(jnp.float32)
    return total


def doc_index(doc_lengths, positions):
    starts = jnp.cumsum(doc_lengths) - doc_lengths
    inside = (starts[None, :] <= positions[:, None]).astype(jnp.int32)
    return jnp.sum(inside, axis=1) - 1


def cost(flops, arrays, transcendentals=0):
    moved = sum(a.size * a.dtype.itemsize for a in arrays)
    return pl.CostEstimate(flops=flops, bytes_accessed=moved, transcendentals=transcendentals)


def dot(lhs, rhs, lhs_dim=1, rhs_dim=0):
    return lax.dot_general(
        lhs, rhs, (((lhs_dim,), (rhs_dim,)), ((), ())), preferred_element_type=jnp.float32
    )


def softmax(scores):
    weights = jnp.exp(scores - jnp.max(scores, axis=-1, keepdims=True))
    return (weights / jnp.sum(weights, axis=-1, keepdims=True)).astype(jnp.bfloat16)


def byte_layer_kernel(
    q_ref, k_ref, v_ref, h_ref, qdoc_ref, kdoc_ref, start_ref, end_ref, present_ref, out_ref, bias_ref
):
    length, reach = q_ref.shape[0], k_ref.shape[0] - q_ref.shape[0]

    @pl.when(pl.program_id(0) == 0)
    def _():
        row = lax.broadcasted_iota(jnp.int32, bias_ref.shape, 0)
        back = row + reach - lax.broadcasted_iota(jnp.int32, bias_ref.shape, 1)
        allowed = (back >= 0) & (back < WINDOW) & (qdoc_ref[...] == kdoc_ref[...])
        bias_ref[...] = jnp.where(allowed, 0.0, masked_score)

    scores = dot(q_ref[...], k_ref[...], 1, 1) / math.sqrt(HEAD)
    weights = softmax(jnp.where(bias_ref[...] == 0.0, scores, masked_score))
    mixed = dot(weights, v_ref[...])
    states = (h_ref[...].astype(jnp.float32) + mixed).astype(jnp.bfloat16)
    present = present_ref[...] > 0
    ids = lax.broadcasted_iota(jnp.int32, (start_ref.shape[0], length), 1)
    member = present & (start_ref[...] <= ids) & (ids < end_ref[...])
    counts = jnp.where(member, 1.0, 0.0)
    sizes = jnp.sum(counts, axis=1, keepdims=True)
    pooled = (dot(counts.astype(jnp.bfloat16), states) / jnp.maximum(sizes, 1.0)).astype(jnp.bfloat16)
    scores = dot(pooled, states, 1, 1) / math.sqrt(HEAD)
    weights = softmax(jnp.where(member, scores, masked_score))
    out_ref[...] = jnp.where(present, dot(weights, states), 0.0).astype(jnp.bfloat16)


def byte_layer(queries, key_all, value_all, states, query_doc, key_doc, offsets, count):
    length, width = queries.shape
    reach = key_all.shape[0]
    slot_count = offsets.shape[0]
    slots = jnp.arange(slot_count, dtype=jnp.int32)
    following = jnp.concatenate([offsets[1:], jnp.full((1,), length, jnp.int32)])
    ends = jnp.where(slots == count - 1, length, following)
    present = (slots < count).astype(jnp.int32)

    def head(rows):
        return pl.BlockSpec((rows, HEAD), lambda i: (0, i))

    def whole(shape):
        return pl.BlockSpec(shape, lambda i: (0, 0))

    column = whole((slot_count, 1))
    return pl.pallas_call(
        byte_layer_kernel,
        grid=(width // HEAD,),
        in_specs=[
            head(length),
            head(reach),
            head(reach),
            head(length),
            whole((length, 1)),
            whole((1, reach)),
            column,
            column,
            column,
        ],
        out_specs=head(slot_count),
        out_shape=jax.ShapeDtypeStruct((slot_count, width), jnp.bfloat16),
        scratch_shapes=[pltpu.VMEM((length, reach), jnp.float32)],
        cost_estimate=cost(4 * length * reach * width, (queries, key_all, value_all, states)),
        name="byte_layer",
    )(
        queries,
        key_all,
        value_all,
        states,
        query_doc[:, None],
        key_doc[None, :],
        offsets[:, None],
        ends[:, None],
        present[:, None],
    )


def tile(count):
    return 256 if count % 256 == 0 else count


def product(lhs_ref, weight_refs):
    depth = weight_refs[0].shape[0]
    total = None
    for k, ref in enumerate(weight_refs):
        term = dot(lhs_ref[:, k * depth : (k + 1) * depth], ref[...])
        total = term if total is None else total + term
    return total


def weight_specs(pieces, low, wide):
    return [pl.BlockSpec((piece.shape[0], wide), lambda i: (0, low // wide)) for piece in pieces]


def partial_sums(lhs, pieces, low, wide):
    def kernel(lhs_ref, *refs):
        refs[-1][...] = product(lhs_ref, refs[:-1]).astype(jnp.bfloat16)

    rows, depth = lhs.shape
    step = tile(rows)
    out = jax.ShapeDtypeStruct((rows, wide), jnp.bfloat16)
    return pl.pallas_call(
        kernel,
        grid=(rows // step,),
        in_specs=[pl.BlockSpec((step, depth), lambda i: (i, 0))] + weight_specs(pieces, low, wide),
        out_specs=pl.BlockSpec((step, wide), lambda i: (i, 0)),
        out_shape=out,
        cost_estimate=cost(2 * rows * depth * wide, (lhs, out, out)),
        name="partial_sums",
    )(lhs, *pieces)


def gates(lhs, pieces, low, wide, received, cotangents, start):
    width = wide // 2

    def kernel(lhs_ref, *refs):
        refs, (cot_ref, hidden_ref, grad_ref) = refs[:-3], refs[-3:]
        pre = product(lhs_ref, refs[: len(pieces)])
        for ref in refs[len(pieces) :]:
            pre = pre + ref[...].astype(jnp.float32)
        gate_pre, up_pre = pre[:, :width], pre[:, width:]
        cotangent = cot_ref[...].astype(jnp.float32)
        sigmoid_gate = jax.nn.sigmoid(gate_pre)
        hidden_ref[...] = (gate_pre * sigmoid_gate * up_pre).astype(jnp.bfloat16)
        gate_grad = cotangent * up_pre * sigmoid_gate * (1.0 + gate_pre * (1.0 - sigmoid_gate))
        grad_ref[:, :width] = gate_grad.astype(jnp.bfloat16)
        grad_ref[:, width:] = (cotangent * gate_pre * sigmoid_gate).astype(jnp.bfloat16)

    rows, depth = lhs.shape
    step = tile(rows)
    across = pl.BlockSpec((step, wide), lambda i: (i, 0))
    return pl.pallas_call(
        kernel,
        grid=(rows // step,),
        in_specs=[pl.BlockSpec((step, depth), lambda i: (i, 0))]
        + weight_specs(pieces, low, wide)
        + [across] * len(received)
        + [pl.BlockSpec((step, width), lambda i: (i, start // width))],
        out_specs=(pl.BlockSpec((step, width), lambda i: (i, 0)), across),
        out_shape=(
            jax.ShapeDtypeStruct((rows, width), jnp.bfloat16),
            jax.ShapeDtypeStruct((rows, wide), jnp.bfloat16),
        ),
        cost_estimate=cost(2 * rows * depth * wide, (lhs, *received)),
        name="gates",
    )(lhs, *pieces, *received, cotangents)


def outer_sums(lhs_parts, grad_parts, first, count, received, first_received, dtype):
    parts = len(lhs_parts)
    rows, wide = grad_parts[0].shape
    step = tile(count)

    def kernel(*refs):
        total = None
        for k in range(parts):
            term = dot(refs[k][...], refs[parts + k][...], 0, 0)
            total = term if total is None else total + term
        for ref in refs[2 * parts : -1]:
            total = total + ref[...].astype(jnp.float32)
        refs[-1][...] = total.astype(dtype)

    out = jax.ShapeDtypeStruct((count, wide), dtype)
    return pl.pallas_call(
        kernel,
        grid=(count // step,),
        in_specs=[pl.BlockSpec((rows, step), lambda i: (0, first // step + i))] * parts
        + [pl.BlockSpec((rows, wide), lambda i: (0, 0))] * parts
        + [pl.BlockSpec((step, wide), lambda i: (first_received // step + i, 0))] * len(received),
        out_specs=pl.BlockSpec((step, wide), lambda i: (i, 0)),
        out_shape=out,
        cost_estimate=cost(2 * rows * parts * count * wide, (*grad_parts, out, out)),
        name="outer_sums",
    )(*lhs_parts, *grad_parts, *received)


def input_sums(grads, weights, first, count, before, dtype):
    parts = len(grads[0])
    pieces = len(weights[0][0])
    depth = weights[0][0][0].shape[0]
    step = tile(count)
    chunks = len(grads)
    across = pl.BlockSpec((parts, step, pieces * depth), lambda i: (0, first // step + i, 0))

    def kernel(*refs):
        grad_refs = refs[: parts * chunks]
        weight_refs = refs[parts * chunks : (parts + pieces) * chunks]
        out_ref = refs[-1]
        for k in range(parts):
            for p in range(pieces):
                columns = slice(p * depth, (p + 1) * depth)
                total = refs[-2][k, :, columns] if before is not None else None
                for c in range(chunks):
                    term = dot(
                        grad_refs[c * parts + k][...], weight_refs[c * pieces + p][...], 1, 1
                    )
                    total = term if total is None else total + term
                out_ref[k, :, columns] = total.astype(dtype)

    out = jax.ShapeDtypeStruct((parts, count, pieces * depth), dtype)
    in_specs, operands = [], []
    for chunk in grads:
        for part in chunk:
            in_specs.append(pl.BlockSpec((step, part.shape[1]), lambda i: (first // step + i, 0)))
            operands.append(part)
    for group, low, wide in weights:
        in_specs += weight_specs(group, low, wide)
        operands += group
    if before is not None:
        in_specs.append(across)
        operands.append(before)
    wide = sum(chunk[0].shape[1] for chunk in grads)
    return pl.pallas_call(
        kernel,
        grid=(count // step,),
        in_specs=in_specs,
        out_specs=pl.BlockSpec((parts, step, pieces * depth), lambda i: (0, i, 0)),
        out_shape=out,
        cost_estimate=cost(2 * parts * count * wide * pieces * depth, (out, out)),
        name="input_sums",
    )(*operands)


def shards(
    bytes_in,
    doc_lengths,
    patch_offsets,
    patch_counts,
    w_query,
    w_key,
    w_value,
    w_proj,
    norm_gain,
    gate_w,
    up_w,
    d_hidden,
):
    bf16, f32 = jnp.bfloat16, jnp.float32
    x_count, core_count = (lax.axis_size(axis) for axis in ROW_AXES)
    a_count, c_count, b_count = (lax.axis_size(axis) for axis in COL_AXES)
    x_own, core_own = (lax.axis_index(axis) for axis in ROW_AXES)
    a_own, c_own, b_own = (lax.axis_index(axis) for axis in COL_AXES)
    states = bytes_in[0]
    length = states.shape[0]
    hop_count = (WINDOW - 2 + length) // length
    first_pos = lax.axis_index(ALL_AXES) * length

    earlier = []
    for distance in range(1, hop_count + 1):
        earlier.insert(0, shifted(states, ALL_AXES, distance))
    queries, key_own, value_own = (
        jnp.dot(states, w, preferred_element_type=f32).astype(bf16) for w in (w_query, w_key, w_value)
    )

    rows, units = gate_w.shape
    sub = units // c_count
    spans = [(start, min(CHUNK, sub - start)) for start in range(0, sub, CHUNK)]
    group_size = (len(spans) + 1) // 2
    groups = [spans[:group_size], spans[group_size:]]
    groups = [(g[0][0], g[-1][0] + g[-1][1], g) for g in groups if g]

    def weight_payload(by, members, gate, up):
        parts = [split(w, c_count, 1) for w in (gate, up)]
        return jnp.concatenate(
            [
                chosen([p[:, first : first + width] for p in side], (c_own + by) % c_count)
                for first, width in members
                for side in parts
            ],
            axis=1,
        )

    def weight_pieces(index, gate, up):
        members = groups[index][2]
        pieces = {}
        for c_by in range(c_count):
            payload = weight_payload(c_by, members, gate, up)
            for b_by in range(b_count):
                if c_by and b_by:
                    pairs = [
                        (c * b_count + b, (c + c_by) % c_count * b_count + (b + b_by) % b_count)
                        for c in range(c_count)
                        for b in range(b_count)
                    ]
                    pieces[b_by, c_by] = lax.ppermute(payload, ("c", "b"), pairs)
                elif c_by:
                    pieces[b_by, c_by] = turned(payload, "c", c_by)
                else:
                    pieces[b_by, c_by] = turned(payload, "b", b_by)
        return [pieces[b_by, c_by] for b_by in range(b_count) for c_by in range(c_count)]

    gate_first, up_first, *earlier = lax.optimization_barrier((gate_w, up_w, *earlier))
    pieces = [weight_pieces(0, gate_first, up_first)]

    late = [
        [jnp.dot(part, w, preferred_element_type=f32).astype(bf16) for w in (w_key, w_value)]
        for part in earlier
    ]
    key_all = jnp.concatenate([pair[0] for pair in late] + [key_own])
    value_all = jnp.concatenate([pair[1] for pair in late] + [value_own])
    query_pos = first_pos + jnp.arange(length, dtype=jnp.int32)
    key_pos = first_pos - hop_count * length + jnp.arange((hop_count + 1) * length, dtype=jnp.int32)
    key_doc = doc_index(doc_lengths, key_pos)
    query_doc = key_doc[hop_count * length :]
    context = byte_layer(
        queries, key_all, value_all, states, query_doc, key_doc, patch_offsets[0], patch_counts[0, 0]
    )
    slot_count = context.shape[0]

    features = jnp.dot(context, w_proj, preferred_element_type=f32).astype(bf16)
    own_float = features.astype(f32)
    model_width = own_float.shape[1]
    own_inverse = lax.rsqrt(jnp.mean(own_float * own_float, axis=1, keepdims=True) + epsilon)
    normed = (own_float * own_inverse * norm_gain).astype(bf16)

    part_width = model_width // a_count
    quarter = part_width // b_count
    a_blocks = split(normed, a_count, 1)

    def columns_for(part, c_by):
        blocks = split(part, c_count * b_count, 1)
        wanted = []
        for b in range(b_count):
            for c in range(c_count):
                place = (c_own + c_by - c) % c_count * b_count + (b_own - b) % b_count
                wanted.append(chosen(blocks, place))
        return jnp.concatenate(wanted, axis=1)

    normed_parts, first_rows = [], []
    for a_by in range(a_count):
        part = turned(chosen(a_blocks, (a_own - a_by) % a_count), "a", -a_by)
        part = jnp.concatenate(
            [turned(columns_for(part, c_by), "c", c_by) for c_by in range(c_count)]
        )
        first_rows.append(part)
        part = jnp.concatenate([turned(part, "x", by) for by in range(x_count)])
        part = jnp.concatenate([turned(part, "core", by) for by in range(core_count)])
        normed_parts.append(part)
    row_count = normed_parts[0].shape[0]

    gate_last, up_last, d_hidden, *_ = lax.optimization_barrier(
        (gate_w, up_w, d_hidden, *first_rows)
    )
    cotangents = split(d_hidden.reshape(-1, units), c_count, 1)
    cotangents = [
        turned(chosen(cotangents, (c_own + c_by) % c_count), "c", c_by)
        for c_by in range(c_count)
    ]

    pieces += [weight_pieces(index, gate_last, up_last) for index in range(1, len(groups))]
    weights = []
    for (start, _, members), group in zip(groups, pieces):
        for first, width in members:
            weights.append((group, 2 * (first - start), 2 * width))

    sums = []
    previous = None
    for weight in weights:
        sent = []
        for a_by in range(1, a_count):
            lhs = normed_parts[a_by] if previous is None else after(normed_parts[a_by], previous)
            previous = partial_sums(lhs, *weight)
            sent.append(turned(previous, "a", a_by))
        sums.append(sent)

    def rows_by_place(array):
        parts = split(array, x_count * core_count, 0)
        return [
            chosen(
                parts, (x_own - x_by) % x_count * core_count + (core_own - core_by) % core_count
            )
            for core_by in range(core_count)
            for x_by in range(x_count)
        ]

    by_place = [rows_by_place(after(part, previous)) for part in cotangents]
    cotangents = jnp.concatenate(
        [by_place[c_by][k] for k in range(x_count * core_count) for c_by in range(c_count)]
    )
    hidden_parts, chunk_grads = [], []
    for index, (start, width) in enumerate(spans):
        lhs = after(normed_parts[0], chunk_grads[-1][0] if index else previous)
        hidden_part, grads = gates(lhs, *weights[index], sums[index], cotangents, start)
        hidden_parts.append(hidden_part)
        chunk_grads.append([turned(grads, "a", -by) for by in range(a_count)])

    weight_grads = []
    input_partial = None
    waiting, done = [], None
    for index, weight in enumerate(weights):
        grads_all = chunk_grads[index]
        if done is not None:
            grads_all = [after(part, done) for part in grads_all]
        received = []
        for by in range(1, b_count):
            partial = outer_sums(normed_parts, grads_all, by * quarter, quarter, [], 0, bf16)
            grads_all = [after(part, partial) for part in grads_all]
            received.append(turned(partial, "b", -by))
        mine = [None] * c_count
        for by in [*range(1, c_count), 0]:
            partial = outer_sums(
                normed_parts, grads_all, by * rows, rows, received, by * rows, bf16 if by else f32
            )
            mine[by] = turned(partial, "c", -by)
        weight_grads.append(mine)
        waiting.append((grads_all, weight))
        if index == len(weights) - 1:
            break
        if index >= len(weights) - 2 or len(waiting) >= 2:
            input_partial = input_sums(
                [pair[0] for pair in waiting],
                [pair[1] for pair in waiting],
                0,
                row_count,
                input_partial,
                f32,
            )
            waiting = []
            done = input_partial

    core_rows = row_count // core_count

    def input_rows(k, dtype):
        return input_sums(
            [pair[0] for pair in waiting],
            [pair[1] for pair in waiting],
            k * core_rows,
            core_rows,
            input_partial,
            dtype,
        )

    sent = [turned(input_rows(k, bf16), "core", -k) for k in range(1, core_count)]
    own_rows = input_rows(0, f32)
    for received in sent:
        own_rows = own_rows + received.astype(f32)
    pieces_by_b = []
    for b_by in range(b_count):
        part = own_rows[:, :, b_by * quarter : (b_by + 1) * quarter]
        part = part.reshape(a_count, x_count, c_count * slot_count, quarter)
        order = lambda sent, k: jnp.concatenate(
            [
                split(sent, c_count, 2)[(c + k) % c_count]
                for c in range(c_count)
            ],
            axis=2,
        )
        if b_by % 2 == 0:
            part = own_sum(part, "x", 1).reshape(a_count, c_count * slot_count, quarter)
            part = own_sum(part, "c", 1, order)
        else:
            part = part.reshape(a_count, x_count, c_count, slot_count, quarter)
            part = part.transpose(0, 2, 1, 3, 4).reshape(
                a_count, c_count * x_count * slot_count, quarter
            )
            part = own_sum(part, "c", 1, order)
            part = own_sum(part, "x", 1)
        pieces_by_b.append(
            [part[0]]
            + [turned(part[by].astype(bf16), "a", by).astype(f32) for by in range(1, a_count)]
        )
    columns = []
    for a in range(a_count):
        ranked = []
        for b_by in range(b_count):
            whole = chosen(
                [pieces_by_b[b_by][(-k) % a_count] for k in range(a_count)], (a - a_own) % a_count
            )
            ranked.append(split(whole, c_count, 1))
        for c in range(c_count):
            for b in range(b_count):
                options = [
                    chosen([ranked[b_by][k] for k in range(c_count)], (c_own - c) % c_count)
                    for b_by in range(b_count)
                ]
                columns.append(chosen(options, (b_own - b) % b_count))
    normed_grad = jnp.concatenate(columns, axis=1)
    scaled = norm_gain * normed_grad
    patch_grad = own_inverse * scaled - own_float * (
        own_inverse * own_inverse * own_inverse
    ) * jnp.mean(scaled * own_float, axis=1, keepdims=True)

    hidden_own = jnp.concatenate(hidden_parts, axis=1).reshape(
        core_count * x_count, c_count, slot_count, sub
    )
    hidden_own = [
        after(turned(hidden_own[:, by].reshape(-1, sub), "c", -by), own_rows)
        for by in range(c_count)
    ]
    hidden_rows = [split(part, core_count * x_count, 0) for part in hidden_own]
    hidden = []
    for x in range(x_count):
        for core in range(core_count):
            place = (core_own - core) % core_count * x_count + (x_own - x) % x_count
            parts = [chosen(part, place) for part in hidden_rows]
            hidden.append(
                jnp.concatenate(
                    [chosen(parts, (k - c_own) % c_count) for k in range(c_count)], axis=1
                )
            )
    hidden = jnp.stack(hidden)

    outs = []
    for side in range(2):
        blocks = [
            jnp.concatenate(
                [
                    mine[by][:, side * width : (side + 1) * width].astype(f32)
                    for (start, width), mine in zip(spans, weight_grads)
                ],
                axis=1,
            )
            for by in range(c_count)
        ]
        outs.append(
            jnp.concatenate(
                [chosen(blocks, (k - c_own) % c_count) for k in range(c_count)], axis=1
            )
        )
    return (hidden, outs[0], outs[1], patch_grad[None])


def halved(count):
    return 2 if count % 2 == 0 else 1


def solution(mesh):
    seq_count, fsdp_count = mesh.shape["seq"], mesh.shape["fsdp"]
    core_count = halved(seq_count)

    def step(*args):
        units = args[9].shape[1] // seq_count
        c_count = 2 if fsdp_count % 2 == 0 and units % 256 == 0 else 1
        b_count = 1
        while fsdp_count // c_count % (4 * b_count * b_count) == 0:
            b_count *= 2
        fine = Mesh(
            mesh.devices.reshape(
                seq_count // core_count,
                core_count,
                fsdp_count // (b_count * c_count),
                c_count,
                b_count,
            ),
            ALL_AXES,
        )
        return jax.shard_map(
            shards,
            mesh=fine,
            in_specs=(
                P(ROW_AXES, COL_AXES, None),
                P(),
                P(ROW_AXES, COL_AXES),
                P(ROW_AXES, COL_AXES),
                P(),
                P(),
                P(),
                P(),
                P(),
                P(COL_AXES, ROW_AXES),
                P(COL_AXES, ROW_AXES),
                P(None, COL_AXES, ROW_AXES),
            ),
            out_specs=(
                P(None, COL_AXES, ROW_AXES),
                P(COL_AXES, ROW_AXES),
                P(COL_AXES, ROW_AXES),
                P(ROW_AXES, COL_AXES, None),
            ),
            check_vma=False,
        )(*args)

    return step
```

time: 1010 us -> 514 us (0.51)
  waiting for transfers between devices: 795 us -> 233 us
  Pallas kernels: 0 us -> 118 us
  matrix products: 91 us -> 20.9 us
  blocking collectives: 69.2 us -> 0 us
  starting transfers between devices: 17.5 us -> 73.8 us
  other arithmetic: 9.42 us -> 34 us
  local copies, waits for them, and re-layouts: 17.2 us -> 29.9 us
  between operations: 14.6 us -> 2.33 us
    reduce_scatter x2 -> x0, waiting for transfers between devices: 478 us -> none  [the longest x1 463 us: shards(): lax.psum_scatter(weight_partial.astype(jnp.bfloat16), 'fsdp', scatter_dim...]
    all_gather x2 -> x0, waiting for transfers between devices: 288 us -> none  [the longest x1 194 us: shards(): lax.all_gather(up_w, 'fsdp', axis=0, tiled=True)]
    ppermute x0 -> x38, waiting for transfers between devices: none -> 233 us  [the longest x36 233 us: turned(): lax.ppermute(shard, axis, [(i, (i + by) % devices) for i in range(devices)])]
    pallas_call x0 -> x25, Pallas kernels: none -> 118 us  [the longest x12 43.8 us: outer_sums(): pl.pallas_call(kernel, grid=(count // step,), in_specs=[pl.BlockSpec((row...]
    all_gather x1 -> x0, blocking collectives: 69.2 us -> none  [shards(): shard_part = lax.all_gather(context[None], 'seq', axis=0, tiled=True)]
    ppermute x0 -> x38, starting transfers between devices: none -> 64.3 us  [the longest x36 50.2 us: turned(): lax.ppermute(shard, axis, [(i, (i + by) % devices) for i in range(devices)])]
    dot_general x13 -> x8, matrix products: 83.2 us -> 20.9 us  [the longest x4 8.57 us: shards(): jnp.dot(part, w, preferred_element_type=f32).astype(bf16)]
    ppermute x4 -> x2, waiting for transfers between devices: 26.7 us -> 0.01 us  [shifted(): return lax.ppermute(shard, axis, pairs)]
  transfers between devices with their start and end apart: 8 -> 40, of which waited for: 7 -> 18; matrix products, arithmetic and copies ran while one was open for 7% -> 11% of each run, Pallas kernels for 0% -> 22%
where the time goes in v1:
time: 514 us; the launch traced here: 512 us
  waiting for transfers between devices  233 us (45%)
  Pallas kernels  118 us (23%)
  starting transfers between devices  73.8 us (14%)
  other arithmetic  34 us (7%)
  local copies, waits for them, and re-layouts  29.9 us (6%)
  matrix products  20.9 us (4%)
    ppermute x36, waiting for transfers between devices, turned(): lax.ppermute(shard, axis, [(i, (i + by) % devices) for i in range(devices)])  233 us
    ppermute x36, starting transfers between devices, turned(): lax.ppermute(shard, axis, [(i, (i + by) % devices) for i in range(devices)])  50.2 us
    pallas_call x12, Pallas kernels, outer_sums(): pl.pallas_call(kernel, grid=(count // step,), in_specs=[pl.BlockSpec((row...  43.8 us
    pallas_call x4, Pallas kernels, input_sums(): pl.pallas_call(kernel, grid=(count // step,), in_specs=in_specs, out_spec...  27.5 us
    pallas_call x4, Pallas kernels, gates(): pl.pallas_call(kernel, grid=(rows // step,), in_specs=[pl.BlockSpec((step...  16.7 us
    pallas_call x1, Pallas kernels, byte_layer(): pl.pallas_call(byte_layer_kernel, grid=(width // HEAD,), in_specs=[head(l...  15.4 us
    pallas_call x4, Pallas kernels, partial_sums(): pl.pallas_call(kernel, grid=(rows // step,), in_specs=[pl.BlockSpec((step...  15 us
    unnamed x85, local copies, waits for them, and re-layouts  15 us
  transfers between devices with their start and end apart: 40, of which 18 were waited for; matrix products, arithmetic and copies ran while one was open for 11% of the time, Pallas kernels for 22%

profile of v1, /device:TPU:0, one launch (start us, length us, event | category | flops | bytes accessed | tf_op | source)
XLA Modules:
  0.0 512.2 jit_solution(14116703374806898481)
XLA Ops:
  0.6 6.0 %collective-permute-start.1 = (bf16[256,1280]{1,0:T(8,128)(2,1)}, bf16[256,1280]{1,0:T(8,128)(2,1)}, u32[]{:S(2)}, u32[]{:S(2)}) collective-permute-start(bf16[256,1280]{1,0:T(8,128)(2,1)} %bitcast.79), channel_id=1, source_target_pairs={{0,1},{1,2},{2,3},{3,4},{4,5},{5,6},{6,7},{7,8},{8,9},{9,10},{10,1... | collective-permute-start | bytes 1966088 | tf_op jit(solution)/shard_map/ppermute | solution.py:29
  6.7 3.5 collective-permute-start
  16.7 4.1 convolution_convert_fusion.7.q_ref
  34.2 14.1 %collective-permute-start.11 = (bf16[512,1024]{1,0:T(8,128)(2,1)}, bf16[512,1024]{1,0:T(8,128)(2,1)}, u32[]{:S(2)}, u32[]{:S(2)}) collective-permute-start(bf16[512,1024]{1,0:T(8,128)(2,1)} %pad_maximum_fusion.11), channel_id=1, source_target_pairs={{0,3},{1,2},{2,1},{3,0},{4,7},{5,6},{6,5},{7,4},{8,11},{9,10},{10,... | collective-permute-start | bytes 3145736 | tf_op jit(solution)/shard_map/ppermute | solution.py:370
  50.4 15.4 %byte_layer.1 = bf16[64,1280]{1,0:T(8,128)(2,1)} custom-call(bf16[256,1280]{1,0:T(8,128)(2,1)} %convolution_convert_fusion.7.q_ref, bf16[768,1280]{1,0:T(8,128)(2,1)} %get-tuple-element.166.k_ref, bf16[768,1280]{1,0:T(8,128)(2,1)} %get-tuple-element.167.v_ref, bf16[256,1280]{1,0:T(8,128)(2,1)} %bitcast.81, s32[256,1]{1,0:T(8,128)} %copy.32.qdoc_ref, ...), custom_call_target="tpu_custom_call" | custom-call | flops 1006632960 | bytes 5242880 | tf_op jit(solution)/shard_map/byte_layer/pallas_call | solution.py:131
  65.9 6.1 %multiply_reduce_fusion.1 = (f32[64]{0:T(128)S(1)}, f32[64,4096]{1,0:T(8,128)S(1)}) fusion(bf16[64,1280]{1,0:T(8,128)(2,1)} %byte_layer.1, bf16[1280,4096]{1,0:T(8,128)(2,1)} %param.19), kind=kOutput, calls=%fused_computation.33 | convolution fusion | flops 672137152 | bytes 11698432 | tf_op jit(solution)/shard_map/dot_general | solution.py:395
  72.8 3.1 collective-permute-start.5
  77.7 22.5 %collective-permute-done.5 = bf16[64,2048]{1,0:T(8,128)(2,1)S(1)} collective-permute-done((bf16[64,2048]{1,0:T(8,128)(2,1)S(1)}, bf16[64,2048]{1,0:T(8,128)(2,1)S(1)}, u32[]{:S(2)}, u32[]{:S(2)}) %collective-permute-start.5) | collective-permute-done | bytes 262176 | tf_op jit(solution)/shard_map/ppermute | solution.py:36
  100.3 3.6 collective-permute-start.6
  112.3 8.7 %collective-permute-done.3 = bf16[128,2048]{1,0:T(8,128)(2,1)S(1)} collective-permute-done((bf16[128,2048]{1,0:T(8,128)(2,1)S(1)}, bf16[128,2048]{1,0:T(8,128)(2,1)S(1)}, u32[]{:S(2)}, u32[]{:S(2)}) %collective-permute-start.3) | collective-permute-done | bytes 524320 | tf_op jit(solution)/shard_map/ppermute | solution.py:36
  121.2 10.3 %collective-permute-done.7 = bf16[128,2048]{1,0:T(8,128)(2,1)S(1)} collective-permute-done((bf16[128,2048]{1,0:T(8,128)(2,1)S(1)}, bf16[128,2048]{1,0:T(8,128)(2,1)S(1)}, u32[]{:S(2)}, u32[]{:S(2)}) %collective-permute-start.7) | collective-permute-done | bytes 524320 | tf_op jit(solution)/shard_map/ppermute | solution.py:36
  135.1 3.4 collective-permute-start.13
  143.6 4.0 partial_sums.4
  147.6 4.0 partial_sums.5
  151.6 21.2 %collective-permute-done.13.refs_2_.refs_4_ = bf16[512,768]{1,0:T(8,128)(2,1)S(1)} collective-permute-done((bf16[512,768]{1,0:T(8,128)(2,1)S(1)}, bf16[512,768]{1,0:T(8,128)(2,1)S(1)}, u32[]{:S(2)}, u32[]{:S(2)}) %collective-permute-start.13) | collective-permute-done | bytes 786464 | tf_op jit(solution)/shard_map/ppermute | solution.py:36
  174.9 4.0 partial_sums.6
  178.9 2.9 collective-permute-start.17
  181.9 3.1 partial_sums.7
  189.8 59.2 %collective-permute-done.15.refs_4_ = bf16[512,512]{1,0:T(8,128)(2,1)S(1)} collective-permute-done((bf16[512,512]{1,0:T(8,128)(2,1)}, bf16[512,512]{1,0:T(8,128)(2,1)S(1)}, u32[]{:S(2)}, u32[]{:S(2)}) %collective-permute-start.15) | collective-permute-done | bytes 524320 | tf_op jit(solution)/shard_map/ppermute | solution.py:36
  249.8 4.5 gates.4
  255.1 4.5 gates.5
  259.6 2.9 collective-permute-start.22
  263.4 4.5 gates.6
  270.7 52.7 %collective-permute-done.19.refs_4_ = bf16[512,256]{1,0:T(8,128)(2,1)S(1)} collective-permute-done((bf16[512,256]{1,0:T(8,128)(2,1)S(1)}, bf16[512,256]{1,0:T(8,128)(2,1)S(1)}, u32[]{:S(2)}, u32[]{:S(2)}) %collective-permute-start.19) | collective-permute-done | bytes 262176 | tf_op jit(solution)/shard_map/ppermute | solution.py:36
  324.1 3.3 gates.7
  328.3 4.8 outer_sums.12
  333.8 4.8 outer_sums.13
  338.6 9.5 %input_sums.4.refs_6_ = f32[2,512,2048]{2,1,0:T(8,128)} custom-call(bf16[512,512]{1,0:T(8,128)(2,1)} %get-tuple-element.66.refs_2_.refs_0_, bf16[512,512]{1,0:T(8,128)(2,1)} %copy-done.13, bf16[512,512]{1,0:T(8,128)(2,1)} %get-tuple-element.68.refs_2_, bf16[512,512]{1,0:T(8,128)(2,1)} %copy-done.15, bf16[512,1024]{1,0:T(8,128)(2,1)} %copy-done.2, ...), custom_call_target="tpu_custom_call" | custom-call | flops 4294967296 | bytes 16777216 | tf_op jit(solution)/shard_map/input_sums/pallas_call | solution.py:298
  348.9 4.8 outer_sums.14
  353.7 7.8 %input_sums.5.refs_6_ = f32[2,512,2048]{2,1,0:T(8,128)} custom-call(bf16[512,512]{1,0:T(8,128)(2,1)} %get-tuple-element.72.refs_2_.refs_0_, bf16[512,512]{1,0:T(8,128)(2,1)} %copy-done.14, bf16[512,768]{1,0:T(8,128)(2,1)} %copy-done.3, bf16[512,768]{1,0:T(8,128)(2,1)} %copy-done.5, bf16[512,768]{1,0:T(8,128)(2,1)} %copy-done.6, bf16[512,768]{1,0:T(8,128)(2,1)} %copy-done.4, ...), custom_call_target="tpu_custom_call" | custom-call | flops 2147483648 | bytes 16777216 | tf_op jit(solution)/shard_map/input_sums/pallas_call | solution.py:298
  362.2 4.3 outer_sums.15
  371.6 3.9 collective-permute-start.20
  375.5 4.7 input_sums.7
  380.2 5.5 %input_sums.6 = f32[2,256,2048]{2,1,0:T(8,128)} custom-call(bf16[512,256]{1,0:T(8,128)(2,1)} %get-tuple-element.76.refs_2_.refs_0_, bf16[512,256]{1,0:T(8,128)(2,1)} %copy-done.16, bf16[512,768]{1,0:T(8,128)(2,1)} %copy-done.3, bf16[512,768]{1,0:T(8,128)(2,1)} %copy-done.5, bf16[512,768]{1,0:T(8,128)(2,1)} %copy-done.6, bf16[512,768]{1,0:T(8,128)(2,1)} %copy-done.4, ...), custom_call_target="tpu_custom_call" | custom-call | flops 536870912 | bytes 8388608 | tf_op jit(solution)/shard_map/input_sums/pallas_call | solution.py:298
  397.7 6.3 %collective-permute-done.28.refs_4_ = bf16[1024,512]{1,0:T(8,128)(2,1)S(1)} collective-permute-done((bf16[1024,512]{1,0:T(8,128)(2,1)}, bf16[1024,512]{1,0:T(8,128)(2,1)S(1)}, u32[]{:S(2)}, u32[]{:S(2)}) %collective-permute-start.28) | collective-permute-done | bytes 1048608 | tf_op jit(solution)/shard_map/ppermute | solution.py:36
  405.0 3.2 outer_sums.17
  408.2 3.9 collective-permute-start.29
  412.1 14.4 %collective-permute-done.26.refs_4_ = bf16[1024,512]{1,0:T(8,128)(2,1)S(1)} collective-permute-done((bf16[1024,512]{1,0:T(8,128)(2,1)}, bf16[1024,512]{1,0:T(8,128)(2,1)S(1)}, u32[]{:S(2)}, u32[]{:S(2)}) %collective-permute-start.26) | collective-permute-done | bytes 1048608 | tf_op jit(solution)/shard_map/ppermute | solution.py:36
  427.5 3.2 outer_sums.16
  430.7 3.9 collective-permute-start.27
  434.6 3.3 outer_sums.21
  439.2 8.8 %collective-permute-done.30.refs_4_ = bf16[1024,512]{1,0:T(8,128)(2,1)} collective-permute-done((bf16[1024,512]{1,0:T(8,128)(2,1)}, bf16[1024,512]{1,0:T(8,128)(2,1)}, u32[]{:S(2)}, u32[]{:S(2)}) %collective-permute-start.30) | collective-permute-done | bytes 1048608 | tf_op jit(solution)/shard_map/ppermute | solution.py:36
  448.0 3.2 outer_sums.18
  453.4 3.3 outer_sums.20
  458.0 3.3 outer_sums.22
  481.0 7.3 %collective-permute-done.37 = bf16[2,1,128,1024]{3,2,0,1:T(8,128)(2,1)S(1)} collective-permute-done((bf16[2,1,128,1024]{3,2,0,1:T(8,128)(2,1)S(1)}, bf16[2,1,128,1024]{3,2,0,1:T(8,128)(2,1)S(1)}, u32[]{:S(2)}, u32[]{:S(2)}) %collective-permute-start.37) | collective-permute-done | bytes 524320 | tf_op jit(solution)/shard_map/ppermute | solution.py:36
  491.7 4.0 collective-permute-done.38
  500.1 6.4 %collective-permute-done.39 = bf16[64,1024]{1,0:T(8,128)(2,1)S(1)} collective-permute-done((bf16[64,1024]{1,0:T(8,128)(2,1)S(1)}, bf16[64,1024]{1,0:T(8,128)(2,1)S(1)}, u32[]{:S(2)}, u32[]{:S(2)}) %collective-permute-start.39) | collective-permute-done | bytes 131104 | tf_op jit(solution)/shard_map/ppermute | solution.py:36
  (256 shorter events, 113.8 us)
Async XLA Ops:
  0.6 21.8 %copy-start = (bf16[1280,1280]{1,0:T(8,128)(2,1)S(1)}, bf16[1280,1280]{1,0:T(8,128)(2,1)}, u32[]{:S(2)}) copy-start(bf16[1280,1280]{1,0:T(8,128)(2,1)} %param.18) | copy-start | bytes 9830404
  0.6 22.8 %collective-permute-start.1 = (bf16[256,1280]{1,0:T(8,128)(2,1)}, bf16[256,1280]{1,0:T(8,128)(2,1)}, u32[]{:S(2)}, u32[]{:S(2)}) collective-permute-start(bf16[256,1280]{1,0:T(8,128)(2,1)} %bitcast.79), channel_id=1, source_target_pairs={{0,1},{1,2},{2,3},{3,4},{4,5},{5,6},{6,7},{7,8},{8,9},{9,10},{10,1... | collective-permute-start | bytes 1966088 | tf_op jit(solution)/shard_map/ppermute | solution.py:29
  6.7 16.8 %collective-permute-start = (bf16[256,1280]{1,0:T(8,128)(2,1)}, bf16[256,1280]{1,0:T(8,128)(2,1)}, u32[]{:S(2)}, u32[]{:S(2)}) collective-permute-start(bf16[256,1280]{1,0:T(8,128)(2,1)} %bitcast.80), channel_id=1, source_target_pairs={{0,2},{1,3},{2,4},{3,5},{4,6},{5,7},{6,8},{7,9},{8,10},{9,11},{10,... | collective-permute-start | bytes 1966088 | tf_op jit(solution)/shard_map/ppermute | solution.py:29
  34.2 100.8 %collective-permute-start.11 = (bf16[512,1024]{1,0:T(8,128)(2,1)}, bf16[512,1024]{1,0:T(8,128)(2,1)}, u32[]{:S(2)}, u32[]{:S(2)}) collective-permute-start(bf16[512,1024]{1,0:T(8,128)(2,1)} %pad_maximum_fusion.11), channel_id=1, source_target_pairs={{0,3},{1,2},{2,1},{3,0},{4,7},{5,6},{6,5},{7,4},{8,11},{9,10},{10,... | collective-permute-start | bytes 3145736 | tf_op jit(solution)/shard_map/ppermute | solution.py:370
  48.3 95.3 %collective-permute-start.9 = (bf16[512,1024]{1,0:T(8,128)(2,1)}, bf16[512,1024]{1,0:T(8,128)(2,1)}, u32[]{:S(2)}, u32[]{:S(2)}) collective-permute-start(bf16[512,1024]{1,0:T(8,128)(2,1)} %pad_maximum_fusion.11), channel_id=1, source_target_pairs={{0,2},{2,0},{1,3},{3,1},{4,6},{6,4},{5,7},{7,5},{8,10},{10,8},{9,1... | collective-permute-start | bytes 3145736 | tf_op jit(solution)/shard_map/ppermute | solution.py:36
  72.8 31.1 %copy-start.22 = (bf16[512,256]{1,0:T(8,128)(2,1)S(1)}, bf16[512,256]{1,0:T(8,128)(2,1)}, u32[]{:S(2)}) copy-start(bf16[512,256]{1,0:T(8,128)(2,1)} %get-tuple-element.163) | copy-start | bytes 786436
  72.8 31.1 %copy-start.23 = (bf16[512,256]{1,0:T(8,128)(2,1)S(1)}, bf16[512,256]{1,0:T(8,128)(2,1)}, u32[]{:S(2)}) copy-start(bf16[512,256]{1,0:T(8,128)(2,1)} %get-tuple-element.164) | copy-start | bytes 786436
  72.8 27.3 %collective-permute-start.5 = (bf16[64,2048]{1,0:T(8,128)(2,1)S(1)}, bf16[64,2048]{1,0:T(8,128)(2,1)S(1)}, u32[]{:S(2)}, u32[]{:S(2)}) collective-permute-start(bf16[64,2048]{1,0:T(8,128)(2,1)S(1)} %get-tuple-element.142), channel_id=1, source_target_pairs={{0,4},{4,0},{1,5},{5,1},{2,6},{6,2},{3,7},{7,3},{8,12},{12,8},{9,1... | collective-permute-start | bytes 786440 | tf_op jit(solution)/shard_map/ppermute | solution.py:36
  76.1 29.7 %collective-permute-start.2 = (bf16[64,2048]{1,0:T(8,128)(2,1)S(1)}, bf16[64,2048]{1,0:T(8,128)(2,1)S(1)}, u32[]{:S(2)}, u32[]{:S(2)}) collective-permute-start(bf16[64,2048]{1,0:T(8,128)(2,1)S(1)} %pad_maximum_fusion.21), channel_id=1, source_target_pairs={{0,2},{2,0},{1,3},{3,1},{4,6},{6,4},{5,7},{7,5},{8,10},{10,8},{9,1... | collective-permute-start | bytes 786440 | tf_op jit(solution)/shard_map/ppermute | solution.py:36
  100.3 10.7 %collective-permute-start.6 = (bf16[64,2048]{1,0:T(8,128)(2,1)S(1)}, bf16[64,2048]{1,0:T(8,128)(2,1)S(1)}, u32[]{:S(2)}, u32[]{:S(2)}) collective-permute-start(bf16[64,2048]{1,0:T(8,128)(2,1)S(1)} %pad_maximum_fusion.22), channel_id=1, source_target_pairs={{0,2},{2,0},{1,3},{3,1},{4,6},{6,4},{5,7},{7,5},{8,10},{10,8},{9,1... | collective-permute-start | bytes 786440 | tf_op jit(solution)/shard_map/ppermute | solution.py:36
  104.0 8.3 %copy-start.2 = (bf16[512,1024]{1,0:T(8,128)(2,1)}, bf16[512,1024]{1,0:T(8,128)(2,1)S(1)}, u32[]{:S(2)}) copy-start(bf16[512,1024]{1,0:T(8,128)(2,1)S(1)} %pad_maximum_fusion.10.refs_0_.refs_4_.refs_8_) | copy-start | bytes 3145732
  104.0 31.0 %collective-permute-start.10 = (bf16[512,1024]{1,0:T(8,128)(2,1)S(1)}, bf16[512,1024]{1,0:T(8,128)(2,1)S(1)}, u32[]{:S(2)}, u32[]{:S(2)}) collective-permute-start(bf16[512,1024]{1,0:T(8,128)(2,1)S(1)} %pad_maximum_fusion.10.refs_0_.refs_4_.refs_8_), channel_id=1, source_target_pairs={{0,1},{1,0},{2,3},{3,2},{4,5},{5,4},{6,7},{7,6},{8,9},{9,8},{10,11... | collective-permute-start | bytes 3145736 | tf_op jit(solution)/shard_map/ppermute | solution.py:36
  105.9 15.2 %collective-permute-start.3 = (bf16[128,2048]{1,0:T(8,128)(2,1)S(1)}, bf16[128,2048]{1,0:T(8,128)(2,1)S(1)}, u32[]{:S(2)}, u32[]{:S(2)}) collective-permute-start(bf16[128,2048]{1,0:T(8,128)(2,1)S(1)} %pad_maximum_fusion.18), channel_id=1, source_target_pairs={{0,16},{16,0},{1,17},{17,1},{2,18},{18,2},{3,19},{19,3},{4,20},{20... | collective-permute-start | bytes 1572872 | tf_op jit(solution)/shard_map/ppermute | solution.py:36
  111.1 20.4 %collective-permute-start.7 = (bf16[128,2048]{1,0:T(8,128)(2,1)S(1)}, bf16[128,2048]{1,0:T(8,128)(2,1)S(1)}, u32[]{:S(2)}, u32[]{:S(2)}) collective-permute-start(bf16[128,2048]{1,0:T(8,128)(2,1)S(1)} %pad_maximum_fusion.19), channel_id=1, source_target_pairs={{0,16},{16,0},{1,17},{17,1},{2,18},{18,2},{3,19},{19,3},{4,20},{20... | collective-permute-start | bytes 1572872 | tf_op jit(solution)/shard_map/ppermute | solution.py:36
  121.1 14.0 %collective-permute-start.4 = (bf16[256,2048]{1,0:T(8,128)(2,1)S(1)}, bf16[256,2048]{1,0:T(8,128)(2,1)S(1)}, u32[]{:S(2)}, u32[]{:S(2)}) collective-permute-start(bf16[256,2048]{1,0:T(8,128)(2,1)S(1)} %pad_maximum_fusion.8), channel_id=1, source_target_pairs={{0,8},{8,0},{1,9},{9,1},{2,10},{10,2},{3,11},{11,3},{4,12},{12,4},... | collective-permute-start | bytes 3145736 | tf_op jit(solution)/shard_map/ppermute | solution.py:36
  131.6 9.3 %collective-permute-start.8 = (bf16[256,2048]{1,0:T(8,128)(2,1)S(1)}, bf16[256,2048]{1,0:T(8,128)(2,1)S(1)}, u32[]{:S(2)}, u32[]{:S(2)}) collective-permute-start(bf16[256,2048]{1,0:T(8,128)(2,1)S(1)} %pad_maximum_fusion.9), channel_id=1, source_target_pairs={{0,8},{8,0},{1,9},{9,1},{2,10},{10,2},{3,11},{11,3},{4,12},{12,4},... | collective-permute-start | bytes 3145736 | tf_op jit(solution)/shard_map/ppermute | solution.py:36
  135.0 37.8 %collective-permute-start.14 = (bf16[512,768]{1,0:T(8,128)(2,1)}, bf16[512,768]{1,0:T(8,128)(2,1)S(1)}, u32[]{:S(2)}, u32[]{:S(2)}) collective-permute-start(bf16[512,768]{1,0:T(8,128)(2,1)} %pad_maximum_fusion.17), channel_id=1, source_target_pairs={{0,3},{1,2},{2,1},{3,0},{4,7},{5,6},{6,5},{7,4},{8,11},{9,10},{10,... | collective-permute-start | bytes 2359304 | tf_op jit(solution)/shard_map/ppermute | solution.py:370
  135.0 37.8 %collective-permute-start.12 = (bf16[512,768]{1,0:T(8,128)(2,1)}, bf16[512,768]{1,0:T(8,128)(2,1)S(1)}, u32[]{:S(2)}, u32[]{:S(2)}) collective-permute-start(bf16[512,768]{1,0:T(8,128)(2,1)} %pad_maximum_fusion.17), channel_id=1, source_target_pairs={{0,2},{2,0},{1,3},{3,1},{4,6},{6,4},{5,7},{7,5},{8,10},{10,8},{9,1... | collective-permute-start | bytes 2359304 | tf_op jit(solution)/shard_map/ppermute | solution.py:36
  135.1 37.7 %collective-permute-start.13 = (bf16[512,768]{1,0:T(8,128)(2,1)S(1)}, bf16[512,768]{1,0:T(8,128)(2,1)S(1)}, u32[]{:S(2)}, u32[]{:S(2)}) collective-permute-start(bf16[512,768]{1,0:T(8,128)(2,1)S(1)} %pad_maximum_fusion.16.refs_0_.refs_2_), channel_id=1, source_target_pairs={{0,1},{1,0},{2,3},{3,2},{4,5},{5,4},{6,7},{7,6},{8,9},{9,8},{10,11... | collective-permute-start | bytes 2359304 | tf_op jit(solution)/shard_map/ppermute | solution.py:36
  141.0 44.0 %collective-permute-start.16 = (bf16[256,896]{1,0:T(8,128)(2,1)}, bf16[256,896]{1,0:T(8,128)(2,1)}, u32[]{:S(2)}, u32[]{:S(2)}) collective-permute-start(bf16[256,896]{1,0:T(8,128)(2,1)} %get-tuple-element.126), channel_id=1, source_target_pairs={{0,2},{2,0},{1,3},{3,1},{4,6},{6,4},{5,7},{7,5},{8,10},{10,8},{9,1... | collective-permute-start | bytes 1376264 | tf_op jit(solution)/shard_map/ppermute | solution.py:36
  178.9 83.7 %collective-permute-start.18 = (bf16[512,512]{1,0:T(8,128)(2,1)}, bf16[512,512]{1,0:T(8,128)(2,1)S(1)}, u32[]{:S(2)}, u32[]{:S(2)}) collective-permute-start(bf16[512,512]{1,0:T(8,128)(2,1)} %partial_sums.6), channel_id=1, source_target_pairs={{0,4},{4,0},{1,5},{5,1},{2,6},{6,2},{3,7},{7,3},{8,12},{12,8},{9,1... | collective-permute-start | bytes 1572872 | tf_op jit(solution)/shard_map/ppermute | solution.py:36
  178.9 75.4 %collective-permute-start.17 = (bf16[512,512]{1,0:T(8,128)(2,1)}, bf16[512,512]{1,0:T(8,128)(2,1)S(1)}, u32[]{:S(2)}, u32[]{:S(2)}) collective-permute-start(bf16[512,512]{1,0:T(8,128)(2,1)} %partial_sums.5), channel_id=1, source_target_pairs={{0,4},{4,0},{1,5},{5,1},{2,6},{6,2},{3,7},{7,3},{8,12},{12,8},{9,1... | collective-permute-start | bytes 1572872 | tf_op jit(solution)/shard_map/ppermute | solution.py:36
  181.8 67.2 %collective-permute-start.15 = (bf16[512,512]{1,0:T(8,128)(2,1)}, bf16[512,512]{1,0:T(8,128)(2,1)S(1)}, u32[]{:S(2)}, u32[]{:S(2)}) collective-permute-start(bf16[512,512]{1,0:T(8,128)(2,1)} %partial_sums.4), channel_id=1, source_target_pairs={{0,4},{4,0},{1,5},{5,1},{2,6},{6,2},{3,7},{7,3},{8,12},{12,8},{9,1... | collective-permute-start | bytes 1572872 | tf_op jit(solution)/shard_map/ppermute | solution.py:36
  189.8 59.2 %copy-start.11 = (bf16[512,896]{1,0:T(8,128)(2,1)}, bf16[512,896]{1,0:T(8,128)(2,1)S(1)}, u32[]{:S(2)}) copy-start(bf16[512,896]{1,0:T(8,128)(2,1)S(1)} %select_dynamic-update-slice_fusion.8.refs_5_) | copy-start | bytes 2752516
  254.3 8.2 %copy-start.35 = (bf16[512,256]{1,0:T(8,128)(2,1)S(1)}, bf16[512,256]{1,0:T(8,128)(2,1)}, u32[]{:S(2)}) copy-start(bf16[512,256]{1,0:T(8,128)(2,1)} %partial_sums.7) | copy-start | bytes 786436
  254.3 73.2 %collective-permute-start.21 = (bf16[512,512]{1,0:T(8,128)(2,1)}, bf16[512,512]{1,0:T(8,128)(2,1)S(1)}, u32[]{:S(2)}, u32[]{:S(2)}) collective-permute-start(bf16[512,512]{1,0:T(8,128)(2,1)} %get-tuple-element.66.refs_2_.refs_0_), channel_id=1, source_target_pairs={{0,4},{4,0},{1,5},{5,1},{2,6},{6,2},{3,7},{7,3},{8,12},{12,8},{9,1... | collective-permute-start | bytes 1572872 | tf_op jit(solution)/shard_map/ppermute | solution.py:36
  259.6 73.4 %collective-permute-start.22 = (bf16[512,512]{1,0:T(8,128)(2,1)}, bf16[512,512]{1,0:T(8,128)(2,1)S(1)}, u32[]{:S(2)}, u32[]{:S(2)}) collective-permute-start(bf16[512,512]{1,0:T(8,128)(2,1)} %get-tuple-element.68.refs_2_), channel_id=1, source_target_pairs={{0,4},{4,0},{1,5},{5,1},{2,6},{6,2},{3,7},{7,3},{8,12},{12,8},{9,1... | collective-permute-start | bytes 1572872 | tf_op jit(solution)/shard_map/ppermute | solution.py:36
  262.5 60.9 %collective-permute-start.19 = (bf16[512,256]{1,0:T(8,128)(2,1)S(1)}, bf16[512,256]{1,0:T(8,128)(2,1)S(1)}, u32[]{:S(2)}, u32[]{:S(2)}) collective-permute-start(bf16[512,256]{1,0:T(8,128)(2,1)S(1)} %copy-done.35), channel_id=1, source_target_pairs={{0,4},{4,0},{1,5},{5,1},{2,6},{6,2},{3,7},{7,3},{8,12},{12,8},{9,1... | collective-permute-start | bytes 786440 | tf_op jit(solution)/shard_map/ppermute | solution.py:36
  267.9 80.2 %collective-permute-start.23 = (bf16[512,512]{1,0:T(8,128)(2,1)}, bf16[512,512]{1,0:T(8,128)(2,1)S(1)}, u32[]{:S(2)}, u32[]{:S(2)}) collective-permute-start(bf16[512,512]{1,0:T(8,128)(2,1)} %get-tuple-element.72.refs_2_.refs_0_), channel_id=1, source_target_pairs={{0,4},{4,0},{1,5},{5,1},{2,6},{6,2},{3,7},{7,3},{8,12},{12,8},{9,1... | collective-permute-start | bytes 1572872 | tf_op jit(solution)/shard_map/ppermute | solution.py:36
  327.4 34.1 %collective-permute-start.24 = (bf16[512,256]{1,0:T(8,128)(2,1)}, bf16[512,256]{1,0:T(8,128)(2,1)S(1)}, u32[]{:S(2)}, u32[]{:S(2)}) collective-permute-start(bf16[512,256]{1,0:T(8,128)(2,1)} %get-tuple-element.76.refs_2_.refs_0_), channel_id=1, source_target_pairs={{0,4},{4,0},{1,5},{5,1},{2,6},{6,2},{3,7},{7,3},{8,12},{12,8},{9,1... | collective-permute-start | bytes 786440 | tf_op jit(solution)/shard_map/ppermute | solution.py:36
  361.5 7.8 %copy-start.31 = (bf16[512,256]{1,0:T(8,128)(2,1)S(1)}, bf16[512,256]{1,0:T(8,128)(2,1)}, u32[]{:S(2)}) copy-start(bf16[512,256]{1,0:T(8,128)(2,1)} %get-tuple-element.55) | copy-start | bytes 786436
  361.5 7.8 %copy-start.32 = (bf16[512,256]{1,0:T(8,128)(2,1)S(1)}, bf16[512,256]{1,0:T(8,128)(2,1)}, u32[]{:S(2)}) copy-start(bf16[512,256]{1,0:T(8,128)(2,1)} %get-tuple-element.58) | copy-start | bytes 786436
  366.5 19.2 %collective-permute-start.32 = (bf16[1024,256]{1,0:T(8,128)(2,1)}, bf16[1024,256]{1,0:T(8,128)(2,1)S(1)}, u32[]{:S(2)}, u32[]{:S(2)}) collective-permute-start(bf16[1024,256]{1,0:T(8,128)(2,1)} %outer_sums.15), channel_id=1, source_target_pairs={{0,1},{1,0},{2,3},{3,2},{4,5},{5,4},{6,7},{7,6},{8,9},{9,8},{10,11... | collective-permute-start | bytes 1572872 | tf_op jit(solution)/shard_map/ppermute | solution.py:36
  367.2 36.7 %collective-permute-start.28 = (bf16[1024,512]{1,0:T(8,128)(2,1)}, bf16[1024,512]{1,0:T(8,128)(2,1)S(1)}, u32[]{:S(2)}, u32[]{:S(2)}) collective-permute-start(bf16[1024,512]{1,0:T(8,128)(2,1)} %outer_sums.13), channel_id=1, source_target_pairs={{0,1},{1,0},{2,3},{3,2},{4,5},{5,4},{6,7},{7,6},{8,9},{9,8},{10,11... | collective-permute-start | bytes 3145736 | tf_op jit(solution)/shard_map/ppermute | solution.py:36
  368.5 57.9 %collective-permute-start.26 = (bf16[1024,512]{1,0:T(8,128)(2,1)}, bf16[1024,512]{1,0:T(8,128)(2,1)S(1)}, u32[]{:S(2)}, u32[]{:S(2)}) collective-permute-start(bf16[1024,512]{1,0:T(8,128)(2,1)} %outer_sums.12), channel_id=1, source_target_pairs={{0,1},{1,0},{2,3},{3,2},{4,5},{5,4},{6,7},{7,6},{8,9},{9,8},{10,11... | collective-permute-start | bytes 3145736 | tf_op jit(solution)/shard_map/ppermute | solution.py:36
  369.4 78.7 %collective-permute-start.30 = (bf16[1024,512]{1,0:T(8,128)(2,1)}, bf16[1024,512]{1,0:T(8,128)(2,1)}, u32[]{:S(2)}, u32[]{:S(2)}) collective-permute-start(bf16[1024,512]{1,0:T(8,128)(2,1)} %outer_sums.14), channel_id=1, source_target_pairs={{0,1},{1,0},{2,3},{3,2},{4,5},{5,4},{6,7},{7,6},{8,9},{9,8},{10,11... | collective-permute-start | bytes 3145736 | tf_op jit(solution)/shard_map/ppermute | solution.py:36
  371.6 103.9 %collective-permute-start.20 = (bf16[256,896]{1,0:T(8,128)(2,1)}, bf16[256,896]{1,0:T(8,128)(2,1)S(1)}, u32[]{:S(2)}, u32[]{:S(2)}) collective-permute-start(bf16[256,896]{1,0:T(8,128)(2,1)} %bitcast.9), channel_id=1, source_target_pairs={{0,2},{2,0},{1,3},{3,1},{4,6},{6,4},{5,7},{7,5},{8,10},{10,8},{9,1... | collective-permute-start | bytes 1376264 | tf_op jit(solution)/shard_map/ppermute | solution.py:36
  389.3 6.7 %collective-permute-start.33 = (bf16[512,256]{1,0:T(8,128)(2,1)}, bf16[512,256]{1,0:T(8,128)(2,1)}, u32[]{:S(2)}, u32[]{:S(2)}) collective-permute-start(bf16[512,256]{1,0:T(8,128)(2,1)} %outer_sums.19), channel_id=1, source_target_pairs={{0,2},{2,0},{1,3},{3,1},{4,6},{6,4},{5,7},{7,5},{8,10},{10,8},{9,1... | collective-permute-start | bytes 786440 | tf_op jit(solution)/shard_map/ppermute | solution.py:36
  396.0 75.4 %collective-permute-start.25 = (bf16[2,256,2048]{2,1,0:T(8,128)(2,1)}, bf16[2,256,2048]{2,1,0:T(8,128)(2,1)}, u32[]{:S(2)}, u32[]{:S(2)}) collective-permute-start(bf16[2,256,2048]{2,1,0:T(8,128)(2,1)} %input_sums.7), channel_id=1, source_target_pairs={{0,8},{8,0},{1,9},{9,1},{2,10},{10,2},{3,11},{11,3},{4,12},{12,4},... | collective-permute-start | bytes 6291464 | tf_op jit(solution)/shard_map/ppermute | solution.py:36
  408.2 54.4 %collective-permute-start.29 = (bf16[512,512]{1,0:T(8,128)(2,1)}, bf16[512,512]{1,0:T(8,128)(2,1)}, u32[]{:S(2)}, u32[]{:S(2)}) collective-permute-start(bf16[512,512]{1,0:T(8,128)(2,1)} %outer_sums.17), channel_id=1, source_target_pairs={{0,2},{2,0},{1,3},{3,1},{4,6},{6,4},{5,7},{7,5},{8,10},{10,8},{9,1... | collective-permute-start | bytes 1572872 | tf_op jit(solution)/shard_map/ppermute | solution.py:36
  430.7 33.1 %collective-permute-start.27 = (bf16[512,512]{1,0:T(8,128)(2,1)}, bf16[512,512]{1,0:T(8,128)(2,1)}, u32[]{:S(2)}, u32[]{:S(2)}) collective-permute-start(bf16[512,512]{1,0:T(8,128)(2,1)} %outer_sums.16), channel_id=1, source_target_pairs={{0,2},{2,0},{1,3},{3,1},{4,6},{6,4},{5,7},{7,5},{8,10},{10,8},{9,1... | collective-permute-start | bytes 1572872 | tf_op jit(solution)/shard_map/ppermute | solution.py:36
  451.2 13.6 %collective-permute-start.31 = (bf16[512,512]{1,0:T(8,128)(2,1)}, bf16[512,512]{1,0:T(8,128)(2,1)}, u32[]{:S(2)}, u32[]{:S(2)}) collective-permute-start(bf16[512,512]{1,0:T(8,128)(2,1)} %outer_sums.18), channel_id=1, source_target_pairs={{0,2},{2,0},{1,3},{3,1},{4,6},{6,4},{5,7},{7,5},{8,10},{10,8},{9,1... | collective-permute-start | bytes 1572872 | tf_op jit(solution)/shard_map/ppermute | solution.py:36
  475.9 12.4 %collective-permute-start.37 = (bf16[2,1,128,1024]{3,2,0,1:T(8,128)(2,1)S(1)}, bf16[2,1,128,1024]{3,2,0,1:T(8,128)(2,1)S(1)}, u32[]{:S(2)}, u32[]{:S(2)}) collective-permute-start(bf16[2,1,128,1024]{3,2,0,1:T(8,128)(2,1)S(1)} %copy.43), channel_id=1, source_target_pairs={{0,16},{16,0},{1,17},{17,1},{2,18},{18,2},{3,19},{19,3},{4,20},{20... | collective-permute-start | bytes 1572872 | tf_op jit(solution)/shard_map/ppermute | solution.py:36
  477.9 13.3 %collective-permute-start.34 = (bf16[2,128,1024]{2,1,0:T(8,128)(2,1)S(1)}, bf16[2,128,1024]{2,1,0:T(8,128)(2,1)S(1)}, u32[]{:S(2)}, u32[]{:S(2)}) collective-permute-start(bf16[2,128,1024]{2,1,0:T(8,128)(2,1)S(1)} %pad_maximum_fusion.20), channel_id=1, source_target_pairs={{0,2},{2,0},{1,3},{3,1},{4,6},{6,4},{5,7},{7,5},{8,10},{10,8},{9,1... | collective-permute-start | bytes 1572872 | tf_op jit(solution)/shard_map/ppermute | solution.py:36
  488.6 7.1 %collective-permute-start.38 = (bf16[2,64,1024]{2,1,0:T(8,128)(2,1)S(1)}, bf16[2,64,1024]{2,1,0:T(8,128)(2,1)S(1)}, u32[]{:S(2)}, u32[]{:S(2)}) collective-permute-start(bf16[2,64,1024]{2,1,0:T(8,128)(2,1)S(1)} %pad_maximum_fusion.23), channel_id=1, source_target_pairs={{0,2},{2,0},{1,3},{3,1},{4,6},{6,4},{5,7},{7,5},{8,10},{10,8},{9,1... | collective-permute-start | bytes 786440 | tf_op jit(solution)/shard_map/ppermute | solution.py:36
  491.4 6.4 %collective-permute-start.35 = (bf16[2,64,1024]{2,1,0:T(8,128)(2,1)S(1)}, bf16[2,64,1024]{2,1,0:T(8,128)(2,1)S(1)}, u32[]{:S(2)}, u32[]{:S(2)}) collective-permute-start(bf16[2,64,1024]{2,1,0:T(8,128)(2,1)S(1)} %split.448), channel_id=1, source_target_pairs={{0,16},{16,0},{1,17},{17,1},{2,18},{18,2},{3,19},{19,3},{4,20},{20... | collective-permute-start | bytes 786440 | tf_op jit(solution)/shard_map/ppermute | solution.py:36
  495.8 10.7 %collective-permute-start.39 = (bf16[64,1024]{1,0:T(8,128)(2,1)S(1)}, bf16[64,1024]{1,0:T(8,128)(2,1)S(1)}, u32[]{:S(2)}, u32[]{:S(2)}) collective-permute-start(bf16[64,1024]{1,0:T(8,128)(2,1)S(1)} %fusion.3), channel_id=1, source_target_pairs={{0,4},{4,0},{1,5},{5,1},{2,6},{6,2},{3,7},{7,3},{8,12},{12,8},{9,1... | collective-permute-start | bytes 393224 | tf_op jit(solution)/shard_map/ppermute | solution.py:36
  497.9 10.6 %collective-permute-start.36 = (bf16[64,1024]{1,0:T(8,128)(2,1)S(1)}, bf16[64,1024]{1,0:T(8,128)(2,1)S(1)}, u32[]{:S(2)}, u32[]{:S(2)}) collective-permute-start(bf16[64,1024]{1,0:T(8,128)(2,1)S(1)} %fusion.2), channel_id=1, source_target_pairs={{0,4},{4,0},{1,5},{5,1},{2,6},{6,2},{3,7},{7,3},{8,12},{12,8},{9,1... | collective-permute-start | bytes 393224 | tf_op jit(solution)/shard_map/ppermute | solution.py:36
  (34 other events, 91.2 us)
